TPU v7x, 32 devices: a whole 2x2x4 slice. The times are simulated.
32 devices in a mesh: gx: 4 (over z), gy: 8 (over y, x, core).
Axes of the slice: x: 2, y: 2, z: 4, core: 2. Of those that a mesh axis runs over, the one named last changes fastest.
Arguments:
- rhs: float32 [4, 8, 1, 3, 200, 128], P('gx', 'gy'), may hold values from -25 to 25
- stiff_inverse: bfloat16 [4, 8, 1, 1200, 1200], P('gx', 'gy'), may hold values from -2 to 6, as said below
- schur: bfloat16 [4, 8, 1, 1200, 1200], P('gx', 'gy'), may hold values from -2 to 6, as said below
- phi: bfloat16 [4, 8, 1, 24, 1200], P('gx', 'gy'), may hold values from -0.1875 to 0.1875
- coarse_inverse: float32 [192, 192], P(('gx', 'gy')), may hold values from -2 to 6, as said below
- incidence: int32 [4, 8, 1, 8], P('gx', 'gy'), may hold values from 0 to 63, as said below
- pairing: int32 [4, 8, 1, 3, 200], P('gx', 'gy'), may hold values from 0 to 199, as said below
Outputs:
- multipliers: float32 [4, 8, 1, 3, 200, 128], P('gx', 'gy')
- reduction: float32 [128], replicated
Inputs may be any that keep to these rules, and one draw needn't show every extreme that they name: `stiff_inverse`: each block is symmetric positive definite. `schur`: each block is symmetric positive definite. `coarse_inverse`: symmetric positive definite. `incidence`: the corners of the subdomain grid, periodic in the first two dimensions, under an arbitrary numbering of the 64 nodes: corner c of subdomain (x, y, z) is the grid point (x + c % 2, y + (c // 2) % 2, z + c // 4), and subdomains that share a grid point name the same node. `pairing`: each row over the last dimension is a permutation of 0 to 199.
All inputs are finite; a program needn't handle non-finite values.
Results may differ from a plain program's by a relative error of at most 0.0027.
Values sent between devices are 32-bit elements; how exact they have to be, the bound alone decides.
A program may use at most 64 MiB of HBM per device.

v0:
```python
import jax
import jax.numpy as jnp
from jax import lax
from jax.sharding import PartitionSpec as P

ITERS = 2
largest_index = lax.Precision.HIGHEST


def passed_along(array, axis, by):
    peers = lax.axis_size(axis)
    return lax.ppermute(array, axis, [(i, (i + by) % peers) for i in range(peers)])


def local(rhs, stiff_inverse, schur, phi, coarse_inverse, incidence, pairing):
    blocks = rhs.shape[2]
    face_dofs = rhs.shape[4]
    load_cases = rhs.shape[5]
    interface = 6 * face_dofs
    stiffness = stiff_inverse[0, 0]
    schur_block_stack = schur[0, 0]
    coupling_matrix = phi[0, 0].astype(jnp.float32)
    local_ids = incidence[0, 0]
    level = jnp.arange(blocks)[:, None]
    axis_id = jnp.arange(3)[None, :]
    active = jnp.where((level == blocks - 1) & (axis_id == 2), 0.0, 1.0).astype(jnp.float32)[
        :, :, None, None
    ]
    perm_table = (pairing[0, 0][..., None] == jnp.arange(face_dofs)[None, None, None, :]).astype(
        jnp.float32
    )
    owner_weights = None
    own_ids = jnp.concatenate([local_ids[:, 0], local_ids[-1:, 4]])
    own_dofs = (3 * own_ids[:, None] + jnp.arange(3, dtype=jnp.int32)[None, :]).reshape(-1)
    picked = jnp.take(
        lax.all_gather(coarse_inverse, ("gx", "gy"), axis=0, tiled=True), own_dofs, axis=1
    )
    every_owner = lax.all_gather(own_ids, ("gx", "gy"), axis=0, tiled=True)
    gathered_dofs = (3 * every_owner[:, None] + jnp.arange(3, dtype=jnp.int32)[None, :]).reshape(-1)
    owner_weights = jnp.take(picked, gathered_dofs, axis=0)

    def transpose_jump(values):
        masked = values * active
        moved = jnp.einsum("sakj,sakr->sajr", perm_table, masked, precision=largest_index)
        lower_x = passed_along(moved[:, 0], "gx", 1)
        lower_y = passed_along(moved[:, 1], "gy", 1)
        lower_z = jnp.concatenate([jnp.zeros_like(moved[:1, 2]), moved[:-1, 2]], axis=0)
        return jnp.stack(
            [-lower_x, masked[:, 0], -lower_y, masked[:, 1], -lower_z, masked[:, 2]], axis=1
        )

    def jump_field(field):
        upper_x = passed_along(field[:, 0], "gx", -1)
        upper_y = passed_along(field[:, 2], "gy", -1)
        upper_z = jnp.concatenate([field[1:, 4], jnp.zeros_like(field[:1, 4])], axis=0)
        neighbour = jnp.stack([upper_x, upper_y, upper_z], axis=1)
        paired = jnp.einsum("sakj,sajr->sakr", perm_table, neighbour, precision=largest_index)
        higher = jnp.stack([field[:, 1], field[:, 3], field[:, 5]], axis=1)
        return (higher - paired) * active

    def apply_local(matrices, field):
        low_field = field.reshape(blocks, interface, load_cases).astype(jnp.bfloat16)
        result = jnp.einsum("snm,smr->snr", matrices, low_field, preferred_element_type=jnp.float32)
        return result.reshape(blocks, 6, face_dofs, load_cases)

    def precondition(values):
        field = 0.5 * transpose_jump(values)
        return 0.5 * jump_field(apply_local(schur_block_stack, field))

    def inner_product(left, right):
        return jnp.sum(left * right, axis=(0, 1, 2))

    def energy_total(partial_value):
        return lax.psum(partial_value, ("gx", "gy"))

    residual = rhs[0, 0] * active
    multipliers = jnp.zeros_like(residual)
    preconditioned = precondition(residual)
    partial_energy = inner_product(residual, preconditioned)
    energy = energy_total(partial_energy)
    direction_field = None
    search_corner_values = None
    start_energy = energy
    direction = preconditioned
    for iteration in range(ITERS):
        direction_field = transpose_jump(direction)
        split = jnp.einsum(
            "vzh,vhq->vzq",
            coupling_matrix,
            direction_field.reshape(blocks, interface, load_cases),
            precision=largest_index,
        ).reshape(blocks, 2, 2, 2, 3, load_cases)
        empty = jnp.zeros((1, 2, 2, 3, load_cases), jnp.float32)
        by_node = jnp.concatenate([split[:, 0], empty], axis=0) + jnp.concatenate(
            [empty, split[:, 1]], axis=0
        )
        from_x = passed_along(by_node[:, :, 1], "gx", 1)
        along_x = by_node[:, :, 0] + from_x
        from_y = passed_along(along_x[:, 1], "gy", 1)
        owned = (along_x[:, 0] + from_y).reshape(-1, load_cases)
        gathered = lax.all_gather(owned, ("gx", "gy"), axis=0, tiled=True)
        solved = jnp.dot(owner_weights.T, gathered, precision=largest_index).reshape(
            blocks + 1, 3, load_cases
        )
        from_upper_x = passed_along(solved, "gx", -1)
        pair = jnp.stack([solved, from_upper_x], axis=0)
        from_upper_y = passed_along(pair, "gy", -1)
        quad = jnp.stack([pair, from_upper_y], axis=0)
        neighbour_values = jnp.stack([quad[:, :, :blocks], quad[:, :, 1:]], axis=0)
        neighbour_values = jnp.transpose(neighbour_values, (3, 0, 1, 2, 4, 5)).reshape(
            blocks, -1, load_cases
        )
        search_corner_values = neighbour_values
        spread_operator = jnp.einsum(
            "xgy,xgh->xyh", coupling_matrix, search_corner_values, precision=largest_index
        )
        displacement = apply_local(stiffness, direction_field) + spread_operator.reshape(
            blocks, 6, face_dofs, load_cases
        )
        product_field = jump_field(displacement)
        curvature = lax.psum(inner_product(direction, product_field), ("gx", "gy"))
        alpha = energy / curvature
        multipliers = multipliers + alpha * direction
        residual = residual - alpha * product_field
        preconditioned = precondition(residual)
        partial_energy = inner_product(residual, preconditioned)
        if iteration + 1 < ITERS:
            energy_next = energy_total(partial_energy)
            ratio = energy_next / energy
            direction = preconditioned + ratio * direction
        else:
            energy_next = energy_total(partial_energy)
        energy = energy_next
    return (multipliers[None, None], energy / start_energy)


def solution(mesh):
    return jax.shard_map(
        local,
        mesh=mesh,
        in_specs=(
            P("gx", "gy", None, None, None, None),
            P("gx", "gy", None, None, None),
            P("gx", "gy", None, None, None),
            P("gx", "gy", None, None, None),
            P(("gx", "gy"), None),
            P("gx", "gy", None, None),
            P("gx", "gy", None, None, None),
        ),
        out_specs=(P("gx", "gy", None, None, None, None), P()),
        check_vma=False,
    )
```

profile of v0, /device:TPU:0, one launch (start us, length us, event | category | flops | bytes accessed | tf_op | source)
XLA Modules:
  0.0 463.3 jit_solution(669811901619081959)
XLA Ops:
  4.6 2.6 collective-permute-start
  13.3 40.4 %all-reduce.4 = s32[64]{0:T(128)S(1)} all-reduce(s32[64]{0:T(128)S(1)} %fusion.96), channel_id=1, replica_groups=mesh['gx'=4,'gy'=8] {'gx','gy'}, use_global_device_ids=true, to_apply=%add.4 | all-reduce | flops 64 | bytes 512
  53.9 41.3 %all-gather = f32[32,6,192]{2,1,0:T(8,128)S(1)} all-gather(f32[1,6,192]{2,1,0:T(8,128)} %bitcast.317), channel_id=1, replica_groups=mesh['gx'=4,'gy'=8] {'gx','gy'}, dimensions={0}, use_global_device_ids=true | all-gather | bytes 152064 | tf_op jit(solution)/shard_map/all_gather | solution.py:36
  103.6 2.8 fusion
  106.6 5.0 %collective-permute-done.2 = f32[1,200,128]{2,1,0:T(8,128)S(1)} collective-permute-done((f32[1,200,128]{2,1,0:T(8,128)S(1)}, f32[1,200,128]{2,1,0:T(8,128)S(1)}, u32[]{:S(2)}, u32[]{:S(2)}) %collective-permute-start.2) | collective-permute-done | bytes 102432 | tf_op jit(solution)/shard_map/ppermute | solution.py:12
  114.1 5.6 %collective-permute-done.4 = f32[1,200,128]{2,1,0:T(8,128)S(1)} collective-permute-done((f32[1,200,128]{2,1,0:T(8,128)S(1)}, f32[1,200,128]{2,1,0:T(8,128)S(1)}, u32[]{:S(2)}, u32[]{:S(2)}) %collective-permute-start.4) | collective-permute-done | bytes 102432 | tf_op jit(solution)/shard_map/ppermute | solution.py:12
  121.6 4.9 %collective-permute-done.6 = f32[2,2,3,128]{3,2,1,0:T(4,128)S(1)} collective-permute-done((f32[2,2,3,128]{3,2,1,0:T(4,128)S(1)}, f32[2,2,3,128]{3,2,1,0:T(4,128)S(1)}, u32[]{:S(2)}, u32[]{:S(2)}) %collective-permute-start.6) | collective-permute-done | bytes 6176 | tf_op jit(solution)/shard_map/ppermute | solution.py:12
  132.0 39.4 %all-gather.1 = f32[32,6,128]{2,1,0:T(8,128)} all-gather(f32[1,6,128]{2,1,0:T(8,128)S(1)} %reshape.812), channel_id=1, replica_groups=mesh['gx'=4,'gy'=8] {'gx','gy'}, dimensions={0}, use_global_device_ids=true | all-gather | bytes 101376 | tf_op jit(solution)/shard_map/all_gather | solution.py:101
  173.6 3.6 collective-permute-done.8
  184.4 3.2 collective-permute-start.10
  193.0 38.4 %all-reduce.5 = (f32[128]{0:T(128)S(1)}, f32[128]{0:T(128)S(1)}) all-reduce(f32[128]{0:T(128)S(1)} %get-tuple-element.3, f32[128]{0:T(128)S(1)} %get-tuple-element.2), channel_id=1, replica_groups=mesh['gx'=4,'gy'=8] {'gx','gy'}, use_global_device_ids=true, to_apply=%region_1.2 | all-reduce | flops 256 | bytes 2048 | tf_op jit(solution)/shard_map/psum | solution.py:74
  234.4 2.2 collective-permute-start.12
  236.6 4.3 collective-permute-done.12
  244.5 3.0 collective-permute-done.14
  249.3 39.4 %psum.37 = f32[128]{0:T(128)S(1)} all-reduce(f32[128]{0:T(128)} %get-tuple-element.65), channel_id=1, replica_groups=mesh['gx'=4,'gy'=8] {'gx','gy'}, use_global_device_ids=true, to_apply=%region_5.6 | all-reduce | flops 128 | bytes 1024 | tf_op jit(solution)/shard_map/psum | solution.py:74
  292.7 4.5 collective-permute-done.16
  300.4 4.1 collective-permute-done.18
  304.5 3.9 collective-permute-done.19
  308.4 40.7 %all-gather.2 = f32[32,6,128]{2,1,0:T(8,128)} all-gather(f32[1,6,128]{2,1,0:T(8,128)S(1)} %reshape.814), channel_id=1, replica_groups=mesh['gx'=4,'gy'=8] {'gx','gy'}, dimensions={0}, use_global_device_ids=true | all-gather | bytes 101376 | tf_op jit(solution)/shard_map/all_gather | solution.py:101
  352.0 3.6 collective-permute-done.20
  368.1 38.5 %psum.38 = f32[128]{0:T(128)S(1)} all-reduce(f32[128]{0:T(128)S(1)} %get-tuple-element.67), channel_id=1, replica_groups=mesh['gx'=4,'gy'=8] {'gx','gy'}, use_global_device_ids=true, to_apply=%region_7.8 | all-reduce | flops 128 | bytes 1024 | tf_op jit(solution)/shard_map/psum | solution.py:121
  411.8 4.3 collective-permute-done.24
  419.7 3.0 collective-permute-done.26
  423.2 39.6 %psum.39 = f32[128]{0:T(128)S(1)} all-reduce(f32[128]{0:T(128)S(1)} %fusion.16), channel_id=1, replica_groups=mesh['gx'=4,'gy'=8] {'gx','gy'}, use_global_device_ids=true, to_apply=%region_9.10 | all-reduce | flops 128 | bytes 1024 | tf_op jit(solution)/shard_map/psum | solution.py:74
  (223 shorter events, 83.9 us)
Async XLA Ops:
  4.1 96.7 %collective-permute-start.1 = (f32[1,200,128]{2,1,0:T(8,128)S(1)}, f32[1,200,128]{2,1,0:T(8,128)}, u32[]{:S(2)}, u32[]{:S(2)}) collective-permute-start(f32[1,200,128]{2,1,0:T(8,128)S(1)} %get-tuple-element.47), channel_id=1, source_target_pairs={{0,1},{1,2},{2,3},{3,4},{4,5},{5,6},{6,7},{7,0},{8,9},{9,10},{10,1... | collective-permute-start | bytes 307208 | tf_op jit(solution)/shard_map/ppermute | solution.py:12
  4.6 94.4 %collective-permute-start = (f32[1,200,128]{2,1,0:T(8,128)}, f32[1,200,128]{2,1,0:T(8,128)}, u32[]{:S(2)}, u32[]{:S(2)}) collective-permute-start(f32[1,200,128]{2,1,0:T(8,128)} %get-tuple-element.48), channel_id=1, source_target_pairs={{0,8},{8,16},{16,24},{24,0},{1,9},{9,17},{17,25},{25,1},{2,10},{10... | collective-permute-start | bytes 307208 | tf_op jit(solution)/shard_map/ppermute | solution.py:12
  106.5 5.2 %collective-permute-start.2 = (f32[1,200,128]{2,1,0:T(8,128)S(1)}, f32[1,200,128]{2,1,0:T(8,128)S(1)}, u32[]{:S(2)}, u32[]{:S(2)}) collective-permute-start(f32[1,200,128]{2,1,0:T(8,128)S(1)} %get-tuple-element.34), channel_id=1, source_target_pairs={{0,24},{8,0},{16,8},{24,16},{1,25},{9,1},{17,9},{25,17},{2,26},{10... | collective-permute-start | bytes 307208 | tf_op jit(solution)/shard_map/ppermute | solution.py:12
  106.6 5.1 %collective-permute-start.3 = (f32[1,200,128]{2,1,0:T(8,128)S(1)}, f32[1,200,128]{2,1,0:T(8,128)S(1)}, u32[]{:S(2)}, u32[]{:S(2)}) collective-permute-start(f32[1,200,128]{2,1,0:T(8,128)S(1)} %get-tuple-element.35), channel_id=1, source_target_pairs={{0,7},{1,0},{2,1},{3,2},{4,3},{5,4},{6,5},{7,6},{8,15},{9,8},{10,9... | collective-permute-start | bytes 307208 | tf_op jit(solution)/shard_map/ppermute | solution.py:12
  113.1 6.5 %collective-permute-start.4 = (f32[1,200,128]{2,1,0:T(8,128)S(1)}, f32[1,200,128]{2,1,0:T(8,128)S(1)}, u32[]{:S(2)}, u32[]{:S(2)}) collective-permute-start(f32[1,200,128]{2,1,0:T(8,128)S(1)} %get-tuple-element.46), channel_id=1, source_target_pairs={{0,8},{8,16},{16,24},{24,0},{1,9},{9,17},{17,25},{25,1},{2,10},{10... | collective-permute-start | bytes 307208 | tf_op jit(solution)/shard_map/ppermute | solution.py:12
  113.3 6.4 %collective-permute-start.5 = (f32[1,200,128]{2,1,0:T(8,128)S(1)}, f32[1,200,128]{2,1,0:T(8,128)S(1)}, u32[]{:S(2)}, u32[]{:S(2)}) collective-permute-start(f32[1,200,128]{2,1,0:T(8,128)S(1)} %get-tuple-element.45), channel_id=1, source_target_pairs={{0,1},{1,2},{2,3},{3,4},{4,5},{5,6},{6,7},{7,0},{8,9},{9,10},{10,1... | collective-permute-start | bytes 307208 | tf_op jit(solution)/shard_map/ppermute | solution.py:12
  120.9 5.5 %collective-permute-start.6 = (f32[2,2,3,128]{3,2,1,0:T(4,128)S(1)}, f32[2,2,3,128]{3,2,1,0:T(4,128)S(1)}, u32[]{:S(2)}, u32[]{:S(2)}) collective-permute-start(f32[2,2,3,128]{3,2,1,0:T(4,128)S(1)} %fusion.85), channel_id=1, source_target_pairs={{0,8},{8,16},{16,24},{24,0},{1,9},{9,17},{17,25},{25,1},{2,10},{10... | collective-permute-start | bytes 18440 | tf_op jit(solution)/shard_map/ppermute | solution.py:12
  127.0 4.2 collective-permute-start.7
  173.5 3.7 collective-permute-start.8
  184.4 5.8 %collective-permute-start.10 = (f32[1,200,128]{2,1,0:T(8,128)S(1)}, f32[1,200,128]{2,1,0:T(8,128)S(1)}, u32[]{:S(2)}, u32[]{:S(2)}) collective-permute-start(f32[1,200,128]{2,1,0:T(8,128)S(1)} %get-tuple-element.29), channel_id=1, source_target_pairs={{0,24},{8,0},{16,8},{24,16},{1,25},{9,1},{17,9},{25,17},{2,26},{10... | collective-permute-start | bytes 307208 | tf_op jit(solution)/shard_map/ppermute | solution.py:12
  187.5 4.2 collective-permute-start.11
  234.4 6.5 %collective-permute-start.12 = (f32[1,200,128]{2,1,0:T(8,128)S(1)}, f32[1,200,128]{2,1,0:T(8,128)S(1)}, u32[]{:S(2)}, u32[]{:S(2)}) collective-permute-start(f32[1,200,128]{2,1,0:T(8,128)S(1)} %get-tuple-element.44), channel_id=1, source_target_pairs={{0,8},{8,16},{16,24},{24,0},{1,9},{9,17},{17,25},{25,1},{2,10},{10... | collective-permute-start | bytes 307208 | tf_op jit(solution)/shard_map/ppermute | solution.py:12
  236.6 5.0 %collective-permute-start.13 = (f32[1,200,128]{2,1,0:T(8,128)S(1)}, f32[1,200,128]{2,1,0:T(8,128)S(1)}, u32[]{:S(2)}, u32[]{:S(2)}) collective-permute-start(f32[1,200,128]{2,1,0:T(8,128)S(1)} %get-tuple-element.43), channel_id=1, source_target_pairs={{0,1},{1,2},{2,3},{3,4},{4,5},{5,6},{6,7},{7,0},{8,9},{9,10},{10,1... | collective-permute-start | bytes 307208 | tf_op jit(solution)/shard_map/ppermute | solution.py:12
  242.7 4.7 %collective-permute-start.14 = (f32[1,200,128]{2,1,0:T(8,128)S(1)}, f32[1,200,128]{2,1,0:T(8,128)S(1)}, u32[]{:S(2)}, u32[]{:S(2)}) collective-permute-start(f32[1,200,128]{2,1,0:T(8,128)S(1)} %get-tuple-element.24), channel_id=1, source_target_pairs={{0,24},{8,0},{16,8},{24,16},{1,25},{9,1},{17,9},{25,17},{2,26},{10... | collective-permute-start | bytes 307208 | tf_op jit(solution)/shard_map/ppermute | solution.py:12
  290.7 6.5 %collective-permute-start.16 = (f32[1,200,128]{2,1,0:T(8,128)S(1)}, f32[1,200,128]{2,1,0:T(8,128)S(1)}, u32[]{:S(2)}, u32[]{:S(2)}) collective-permute-start(f32[1,200,128]{2,1,0:T(8,128)S(1)} %get-tuple-element.42), channel_id=1, source_target_pairs={{0,8},{8,16},{16,24},{24,0},{1,9},{9,17},{17,25},{25,1},{2,10},{10... | collective-permute-start | bytes 307208 | tf_op jit(solution)/shard_map/ppermute | solution.py:12
  292.7 5.0 %collective-permute-start.17 = (f32[1,200,128]{2,1,0:T(8,128)S(1)}, f32[1,200,128]{2,1,0:T(8,128)S(1)}, u32[]{:S(2)}, u32[]{:S(2)}) collective-permute-start(f32[1,200,128]{2,1,0:T(8,128)S(1)} %get-tuple-element.41), channel_id=1, source_target_pairs={{0,1},{1,2},{2,3},{3,4},{4,5},{5,6},{6,7},{7,0},{8,9},{9,10},{10,1... | collective-permute-start | bytes 307208 | tf_op jit(solution)/shard_map/ppermute | solution.py:12
  299.0 5.5 %collective-permute-start.18 = (f32[2,2,3,128]{3,2,1,0:T(4,128)S(1)}, f32[2,2,3,128]{3,2,1,0:T(4,128)S(1)}, u32[]{:S(2)}, u32[]{:S(2)}) collective-permute-start(f32[2,2,3,128]{3,2,1,0:T(4,128)S(1)} %fusion.83), channel_id=1, source_target_pairs={{0,8},{8,16},{16,24},{24,0},{1,9},{9,17},{17,25},{25,1},{2,10},{10... | collective-permute-start | bytes 18440 | tf_op jit(solution)/shard_map/ppermute | solution.py:12
  304.5 3.9 collective-permute-start.19
  351.9 3.7 collective-permute-start.20
  360.9 5.3 %collective-permute-start.22 = (f32[1,200,128]{2,1,0:T(8,128)S(1)}, f32[1,200,128]{2,1,0:T(8,128)S(1)}, u32[]{:S(2)}, u32[]{:S(2)}) collective-permute-start(f32[1,200,128]{2,1,0:T(8,128)S(1)} %get-tuple-element.19), channel_id=1, source_target_pairs={{0,24},{8,0},{16,8},{24,16},{1,25},{9,1},{17,9},{25,17},{2,26},{10... | collective-permute-start | bytes 307208 | tf_op jit(solution)/shard_map/ppermute | solution.py:12
  362.8 4.1 collective-permute-start.23
  409.6 6.5 %collective-permute-start.24 = (f32[1,200,128]{2,1,0:T(8,128)S(1)}, f32[1,200,128]{2,1,0:T(8,128)S(1)}, u32[]{:S(2)}, u32[]{:S(2)}) collective-permute-start(f32[1,200,128]{2,1,0:T(8,128)S(1)} %get-tuple-element.40), channel_id=1, source_target_pairs={{0,8},{8,16},{16,24},{24,0},{1,9},{9,17},{17,25},{25,1},{2,10},{10... | collective-permute-start | bytes 307208 | tf_op jit(solution)/shard_map/ppermute | solution.py:12
  411.8 5.0 %collective-permute-start.25 = (f32[1,200,128]{2,1,0:T(8,128)S(1)}, f32[1,200,128]{2,1,0:T(8,128)S(1)}, u32[]{:S(2)}, u32[]{:S(2)}) collective-permute-start(f32[1,200,128]{2,1,0:T(8,128)S(1)} %get-tuple-element.39), channel_id=1, source_target_pairs={{0,1},{1,2},{2,3},{3,4},{4,5},{5,6},{6,7},{7,0},{8,9},{9,10},{10,1... | collective-permute-start | bytes 307208 | tf_op jit(solution)/shard_map/ppermute | solution.py:12
  417.9 4.7 %collective-permute-start.26 = (f32[1,200,128]{2,1,0:T(8,128)S(1)}, f32[1,200,128]{2,1,0:T(8,128)S(1)}, u32[]{:S(2)}, u32[]{:S(2)}) collective-permute-start(f32[1,200,128]{2,1,0:T(8,128)S(1)} %get-tuple-element.14), channel_id=1, source_target_pairs={{0,24},{8,0},{16,8},{24,16},{1,25},{9,1},{17,9},{25,17},{2,26},{10... | collective-permute-start | bytes 307208 | tf_op jit(solution)/shard_map/ppermute | solution.py:12
  (30 other events, 829.7 us)
where the time goes:
time: 465 us; the launch traced here: 463 us
  blocking collectives  318 us (68%)
  waiting for transfers between devices  58.1 us (12%)
  matrix products  24.5 us (5%)
  starting transfers between devices  24.4 us (5%)
  other arithmetic  20.7 us (4%)
  local copies, waits for them, and re-layouts  16.7 us (4%)
    psum x3, blocking collectives, energy_total(): return lax.psum(partial_value, ('gx', 'gy'))  117 us
    all_gather x2, blocking collectives, local(): gathered = lax.all_gather(owned, ('gx', 'gy'), axis=0, tiled=True)  80 us
    ppermute x28, waiting for transfers between devices, passed_along(): lax.ppermute(array, axis, [(i, (i + by) % peers) for i in range(peers)])  58.1 us
    all_gather x1, blocking collectives, local(): lax.all_gather(coarse_inverse, ('gx', 'gy'), axis=0, tiled=True)  41.3 us
    unnamed x1, blocking collectives  40.4 us
    psum x1, blocking collectives, local(): curvature = lax.psum(inner_product(direction, product_field), ('gx', 'gy'))  38.5 us
    ppermute x28, starting transfers between devices, passed_along(): lax.ppermute(array, axis, [(i, (i + by) % peers) for i in range(peers)])  24.4 us
  transfers between devices with their start and end apart: 28, of which 20 were waited for; matrix products, arithmetic and copies ran while one was open for 4% of the time, Pallas kernels for 0%

commit v1 on v0

--- a/solution.py
+++ b/solution.py
@@ -5,6 +5,11 @@
 
 ITERS = 2
 largest_index = lax.Precision.HIGHEST
+
+
+def gather_over(value, axis, dim):
+    sent = jnp.stack([value] * lax.axis_size(axis))
+    return jnp.concatenate(lax.all_to_all(sent, axis, 0, 0), axis=dim)
 
 
 def passed_along(array, axis, by):
@@ -32,9 +37,7 @@
     owner_weights = None
     own_ids = jnp.concatenate([local_ids[:, 0], local_ids[-1:, 4]])
     own_dofs = (3 * own_ids[:, None] + jnp.arange(3, dtype=jnp.int32)[None, :]).reshape(-1)
-    picked = jnp.take(
-        lax.all_gather(coarse_inverse, ("gx", "gy"), axis=0, tiled=True), own_dofs, axis=1
-    )
+    picked = jnp.take(gather_over(coarse_inverse, ("gx", "gy"), 0), own_dofs, axis=1)
     every_owner = lax.all_gather(own_ids, ("gx", "gy"), axis=0, tiled=True)
     gathered_dofs = (3 * every_owner[:, None] + jnp.arange(3, dtype=jnp.int32)[None, :]).reshape(-1)
     owner_weights = jnp.take(picked, gathered_dofs, axis=0)

time: 465 us -> 423 us (0.910)
  blocking collectives: 318 us -> 276 us
  starting transfers between devices: 24.4 us -> 31.9 us
    all_gather x1 -> x0, blocking collectives: 41.3 us -> none  [local(): lax.all_gather(coarse_inverse, ('gx', 'gy'), axis=0, tiled=True)]
    all_to_all x0 -> x1, starting transfers between devices: none -> 7.33 us  [gather_over(): return jnp.concatenate(lax.all_to_all(sent, axis, 0, 0), axis=dim)]
  transfers between devices with their start and end apart: 28 -> 29, of which waited for: 20 -> 20; matrix products, arithmetic and copies ran while one was open for 4% -> 7% of each run, Pallas kernels for 0% -> 0%
where the time goes in v1:
time: 423 us; the launch traced here: 422 us
  blocking collectives  276 us (65%)
  waiting for transfers between devices  53.8 us (13%)
  starting transfers between devices  31.9 us (8%)
  matrix products  25.1 us (6%)
  other arithmetic  22 us (5%)
  local copies, waits for them, and re-layouts  12.1 us (3%)
    psum x3, blocking collectives, energy_total(): return lax.psum(partial_value, ('gx', 'gy'))  118 us
    all_gather x2, blocking collectives, local(): gathered = lax.all_gather(owned, ('gx', 'gy'), axis=0, tiled=True)  79.4 us
    ppermute x28, waiting for transfers between devices, passed_along(): lax.ppermute(array, axis, [(i, (i + by) % peers) for i in range(peers)])  53.8 us
    unnamed x1, blocking collectives  40.2 us
    psum x1, blocking collectives, local(): curvature = lax.psum(inner_product(direction, product_field), ('gx', 'gy'))  38.4 us
    ppermute x28, starting transfers between devices, passed_along(): lax.ppermute(array, axis, [(i, (i + by) % peers) for i in range(peers)])  24.5 us
    dot_general x5, matrix products, apply_local(): jnp.einsum('snm,smr->snr', matrices, low_field, preferred_element_type=jn...  8.7 us
  transfers between devices with their start and end apart: 29, of which 20 were waited for; matrix products, arithmetic and copies ran while one was open for 7% of the time, Pallas kernels for 0%

profile of v1, /device:TPU:0, one launch (start us, length us, event | category | flops | bytes accessed | tf_op | source)
XLA Modules:
  0.0 422.2 jit_solution(13770739794457885355)
XLA Ops:
  2.2 7.3 %all-to-all-start = ((f32[32,6,192]{2,1,0:T(8,128)}), f32[32,6,192]{2,1,0:T(8,128)S(1)}, u32[]{:S(2)}, u32[]{:S(2)}) async-start(f32[32,6,192]{2,1,0:T(8,128)} %stack.234), calls=%async_computation | async-start | bytes 524288 | tf_op jit(solution)/shard_map/all_to_all | solution.py:12
  19.3 40.2 %all-reduce.4 = s32[64]{0:T(128)S(1)} all-reduce(s32[64]{0:T(128)S(1)} %fusion.96), channel_id=1, replica_groups=mesh['gx'=4,'gy'=8] {'gx','gy'}, use_global_device_ids=true, to_apply=%add.4 | all-reduce | flops 64 | bytes 512
  65.2 2.8 fusion
  68.1 2.4 collective-permute-start.2
  76.8 4.6 %collective-permute-done.4 = f32[1,200,128]{2,1,0:T(8,128)S(1)} collective-permute-done((f32[1,200,128]{2,1,0:T(8,128)S(1)}, f32[1,200,128]{2,1,0:T(8,128)S(1)}, u32[]{:S(2)}, u32[]{:S(2)}) %collective-permute-start.4) | collective-permute-done | bytes 102432 | tf_op jit(solution)/shard_map/ppermute | solution.py:17
  85.5 3.7 collective-permute-done.6
  91.6 2.2 collective-permute-done.7
  93.8 38.4 %all-gather = f32[32,6,128]{2,1,0:T(8,128)S(1)} all-gather(f32[1,6,128]{2,1,0:T(8,128)S(1)} %reshape.816), channel_id=1, replica_groups=mesh['gx'=4,'gy'=8] {'gx','gy'}, dimensions={0}, use_global_device_ids=true | all-gather | bytes 101376 | tf_op jit(solution)/shard_map/all_gather | solution.py:104
  133.2 3.6 collective-permute-done.8
  146.3 2.8 collective-permute-done.10
  150.4 38.8 %all-reduce.5 = (f32[128]{0:T(128)S(1)}, f32[128]{0:T(128)S(1)}) all-reduce(f32[128]{0:T(128)S(1)} %get-tuple-element.3, f32[128]{0:T(128)S(1)} %get-tuple-element.2), channel_id=1, replica_groups=mesh['gx'=4,'gy'=8] {'gx','gy'}, use_global_device_ids=true, to_apply=%region_1.2 | all-reduce | flops 256 | bytes 2048 | tf_op jit(solution)/shard_map/psum | solution.py:77
  194.3 4.3 %collective-permute-done.12 = f32[1,200,128]{2,1,0:T(8,128)S(1)} collective-permute-done((f32[1,200,128]{2,1,0:T(8,128)S(1)}, f32[1,200,128]{2,1,0:T(8,128)S(1)}, u32[]{:S(2)}, u32[]{:S(2)}) %collective-permute-start.12) | collective-permute-done | bytes 102432 | tf_op jit(solution)/shard_map/ppermute | solution.py:17
  202.4 3.0 collective-permute-done.14
  207.2 39.5 %psum.37 = f32[128]{0:T(128)} all-reduce(f32[128]{0:T(128)} %get-tuple-element.65), channel_id=1, replica_groups=mesh['gx'=4,'gy'=8] {'gx','gy'}, use_global_device_ids=true, to_apply=%region_5.6 | all-reduce | flops 128 | bytes 1024 | tf_op jit(solution)/shard_map/psum | solution.py:77
  251.2 4.6 %collective-permute-done.16 = f32[1,200,128]{2,1,0:T(8,128)S(1)} collective-permute-done((f32[1,200,128]{2,1,0:T(8,128)S(1)}, f32[1,200,128]{2,1,0:T(8,128)S(1)}, u32[]{:S(2)}, u32[]{:S(2)}) %collective-permute-start.16) | collective-permute-done | bytes 102432 | tf_op jit(solution)/shard_map/ppermute | solution.py:17
  258.9 4.1 collective-permute-done.18
  263.0 3.9 collective-permute-done.19
  267.0 41.1 %all-gather.1 = f32[32,6,128]{2,1,0:T(8,128)} all-gather(f32[1,6,128]{2,1,0:T(8,128)S(1)} %reshape.818), channel_id=1, replica_groups=mesh['gx'=4,'gy'=8] {'gx','gy'}, dimensions={0}, use_global_device_ids=true | all-gather | bytes 101376 | tf_op jit(solution)/shard_map/all_gather | solution.py:104
  310.9 3.6 collective-permute-done.20
  327.1 38.4 %psum.38 = f32[128]{0:T(128)S(1)} all-reduce(f32[128]{0:T(128)S(1)} %get-tuple-element.67), channel_id=1, replica_groups=mesh['gx'=4,'gy'=8] {'gx','gy'}, use_global_device_ids=true, to_apply=%region_7.8 | all-reduce | flops 128 | bytes 1024 | tf_op jit(solution)/shard_map/psum | solution.py:124
  368.5 2.2 collective-permute-start.24
  370.7 4.3 %collective-permute-done.24 = f32[1,200,128]{2,1,0:T(8,128)S(1)} collective-permute-done((f32[1,200,128]{2,1,0:T(8,128)S(1)}, f32[1,200,128]{2,1,0:T(8,128)S(1)}, u32[]{:S(2)}, u32[]{:S(2)}) %collective-permute-start.24) | collective-permute-done | bytes 102432 | tf_op jit(solution)/shard_map/ppermute | solution.py:17
  378.6 3.0 collective-permute-done.26
  382.1 39.5 %psum.39 = f32[128]{0:T(128)S(1)} all-reduce(f32[128]{0:T(128)S(1)} %fusion.16), channel_id=1, replica_groups=mesh['gx'=4,'gy'=8] {'gx','gy'}, use_global_device_ids=true, to_apply=%region_9.10 | all-reduce | flops 128 | bytes 1024 | tf_op jit(solution)/shard_map/psum | solution.py:77
  (219 shorter events, 82.4 us)
Async XLA Ops:
  2.2 82.4 %all-to-all-start = ((f32[32,6,192]{2,1,0:T(8,128)}), f32[32,6,192]{2,1,0:T(8,128)S(1)}, u32[]{:S(2)}, u32[]{:S(2)}) async-start(f32[32,6,192]{2,1,0:T(8,128)} %stack.234), calls=%async_computation | async-start | bytes 524288 | tf_op jit(solution)/shard_map/all_to_all | solution.py:12
  12.8 51.4 %collective-permute-start.1 = (f32[1,200,128]{2,1,0:T(8,128)S(1)}, f32[1,200,128]{2,1,0:T(8,128)}, u32[]{:S(2)}, u32[]{:S(2)}) collective-permute-start(f32[1,200,128]{2,1,0:T(8,128)S(1)} %get-tuple-element.47), channel_id=1, source_target_pairs={{0,1},{1,2},{2,3},{3,4},{4,5},{5,6},{6,7},{7,0},{8,9},{9,10},{10,1... | collective-permute-start | bytes 307208 | tf_op jit(solution)/shard_map/ppermute | solution.py:17
  13.0 50.2 %collective-permute-start = (f32[1,200,128]{2,1,0:T(8,128)}, f32[1,200,128]{2,1,0:T(8,128)}, u32[]{:S(2)}, u32[]{:S(2)}) collective-permute-start(f32[1,200,128]{2,1,0:T(8,128)} %get-tuple-element.48), channel_id=1, source_target_pairs={{0,8},{8,16},{16,24},{24,0},{1,9},{9,17},{17,25},{25,1},{2,10},{10... | collective-permute-start | bytes 307208 | tf_op jit(solution)/shard_map/ppermute | solution.py:17
  68.1 4.7 %collective-permute-start.2 = (f32[1,200,128]{2,1,0:T(8,128)S(1)}, f32[1,200,128]{2,1,0:T(8,128)S(1)}, u32[]{:S(2)}, u32[]{:S(2)}) collective-permute-start(f32[1,200,128]{2,1,0:T(8,128)S(1)} %get-tuple-element.34), channel_id=1, source_target_pairs={{0,24},{8,0},{16,8},{24,16},{1,25},{9,1},{17,9},{25,17},{2,26},{10... | collective-permute-start | bytes 307208 | tf_op jit(solution)/shard_map/ppermute | solution.py:17
  74.8 6.7 %collective-permute-start.4 = (f32[1,200,128]{2,1,0:T(8,128)S(1)}, f32[1,200,128]{2,1,0:T(8,128)S(1)}, u32[]{:S(2)}, u32[]{:S(2)}) collective-permute-start(f32[1,200,128]{2,1,0:T(8,128)S(1)} %get-tuple-element.46), channel_id=1, source_target_pairs={{0,8},{8,16},{16,24},{24,0},{1,9},{9,17},{17,25},{25,1},{2,10},{10... | collective-permute-start | bytes 307208 | tf_op jit(solution)/shard_map/ppermute | solution.py:17
  74.9 6.6 %collective-permute-start.5 = (f32[1,200,128]{2,1,0:T(8,128)S(1)}, f32[1,200,128]{2,1,0:T(8,128)S(1)}, u32[]{:S(2)}, u32[]{:S(2)}) collective-permute-start(f32[1,200,128]{2,1,0:T(8,128)S(1)} %get-tuple-element.45), channel_id=1, source_target_pairs={{0,1},{1,2},{2,3},{3,4},{4,5},{5,6},{6,7},{7,0},{8,9},{9,10},{10,1... | collective-permute-start | bytes 307208 | tf_op jit(solution)/shard_map/ppermute | solution.py:17
  83.4 5.8 %collective-permute-start.6 = (f32[2,2,3,128]{3,2,1,0:T(4,128)}, f32[2,2,3,128]{3,2,1,0:T(4,128)}, u32[]{:S(2)}, u32[]{:S(2)}) collective-permute-start(f32[2,2,3,128]{3,2,1,0:T(4,128)} %fusion.85), channel_id=1, source_target_pairs={{0,8},{8,16},{16,24},{24,0},{1,9},{9,17},{17,25},{25,1},{2,10},{10... | collective-permute-start | bytes 18440 | tf_op jit(solution)/shard_map/ppermute | solution.py:17
  89.9 3.9 collective-permute-start.7
  133.1 3.7 collective-permute-start.8
  143.8 5.3 %collective-permute-start.10 = (f32[1,200,128]{2,1,0:T(8,128)S(1)}, f32[1,200,128]{2,1,0:T(8,128)S(1)}, u32[]{:S(2)}, u32[]{:S(2)}) collective-permute-start(f32[1,200,128]{2,1,0:T(8,128)S(1)} %get-tuple-element.29), channel_id=1, source_target_pairs={{0,24},{8,0},{16,8},{24,16},{1,25},{9,1},{17,9},{25,17},{2,26},{10... | collective-permute-start | bytes 307208 | tf_op jit(solution)/shard_map/ppermute | solution.py:17
  145.7 3.5 collective-permute-start.11
  192.1 6.5 %collective-permute-start.12 = (f32[1,200,128]{2,1,0:T(8,128)S(1)}, f32[1,200,128]{2,1,0:T(8,128)S(1)}, u32[]{:S(2)}, u32[]{:S(2)}) collective-permute-start(f32[1,200,128]{2,1,0:T(8,128)S(1)} %get-tuple-element.44), channel_id=1, source_target_pairs={{0,8},{8,16},{16,24},{24,0},{1,9},{9,17},{17,25},{25,1},{2,10},{10... | collective-permute-start | bytes 307208 | tf_op jit(solution)/shard_map/ppermute | solution.py:17
  194.3 5.0 %collective-permute-start.13 = (f32[1,200,128]{2,1,0:T(8,128)S(1)}, f32[1,200,128]{2,1,0:T(8,128)S(1)}, u32[]{:S(2)}, u32[]{:S(2)}) collective-permute-start(f32[1,200,128]{2,1,0:T(8,128)S(1)} %get-tuple-element.43), channel_id=1, source_target_pairs={{0,1},{1,2},{2,3},{3,4},{4,5},{5,6},{6,7},{7,0},{8,9},{9,10},{10,1... | collective-permute-start | bytes 307208 | tf_op jit(solution)/shard_map/ppermute | solution.py:17
  200.5 4.9 %collective-permute-start.14 = (f32[1,200,128]{2,1,0:T(8,128)S(1)}, f32[1,200,128]{2,1,0:T(8,128)S(1)}, u32[]{:S(2)}, u32[]{:S(2)}) collective-permute-start(f32[1,200,128]{2,1,0:T(8,128)S(1)} %get-tuple-element.24), channel_id=1, source_target_pairs={{0,24},{8,0},{16,8},{24,16},{1,25},{9,1},{17,9},{25,17},{2,26},{10... | collective-permute-start | bytes 307208 | tf_op jit(solution)/shard_map/ppermute | solution.py:17
  249.3 6.5 %collective-permute-start.16 = (f32[1,200,128]{2,1,0:T(8,128)S(1)}, f32[1,200,128]{2,1,0:T(8,128)S(1)}, u32[]{:S(2)}, u32[]{:S(2)}) collective-permute-start(f32[1,200,128]{2,1,0:T(8,128)S(1)} %get-tuple-element.42), channel_id=1, source_target_pairs={{0,8},{8,16},{16,24},{24,0},{1,9},{9,17},{17,25},{25,1},{2,10},{10... | collective-permute-start | bytes 307208 | tf_op jit(solution)/shard_map/ppermute | solution.py:17
  251.2 5.0 %collective-permute-start.17 = (f32[1,200,128]{2,1,0:T(8,128)S(1)}, f32[1,200,128]{2,1,0:T(8,128)S(1)}, u32[]{:S(2)}, u32[]{:S(2)}) collective-permute-start(f32[1,200,128]{2,1,0:T(8,128)S(1)} %get-tuple-element.41), channel_id=1, source_target_pairs={{0,1},{1,2},{2,3},{3,4},{4,5},{5,6},{6,7},{7,0},{8,9},{9,10},{10,1... | collective-permute-start | bytes 307208 | tf_op jit(solution)/shard_map/ppermute | solution.py:17
  257.5 5.5 %collective-permute-start.18 = (f32[2,2,3,128]{3,2,1,0:T(4,128)S(1)}, f32[2,2,3,128]{3,2,1,0:T(4,128)S(1)}, u32[]{:S(2)}, u32[]{:S(2)}) collective-permute-start(f32[2,2,3,128]{3,2,1,0:T(4,128)S(1)} %fusion.83), channel_id=1, source_target_pairs={{0,8},{8,16},{16,24},{24,0},{1,9},{9,17},{17,25},{25,1},{2,10},{10... | collective-permute-start | bytes 18440 | tf_op jit(solution)/shard_map/ppermute | solution.py:17
  263.0 3.9 collective-permute-start.19
  310.8 3.7 collective-permute-start.20
  319.9 5.3 %collective-permute-start.22 = (f32[1,200,128]{2,1,0:T(8,128)S(1)}, f32[1,200,128]{2,1,0:T(8,128)S(1)}, u32[]{:S(2)}, u32[]{:S(2)}) collective-permute-start(f32[1,200,128]{2,1,0:T(8,128)S(1)} %get-tuple-element.19), channel_id=1, source_target_pairs={{0,24},{8,0},{16,8},{24,16},{1,25},{9,1},{17,9},{25,17},{2,26},{10... | collective-permute-start | bytes 307208 | tf_op jit(solution)/shard_map/ppermute | solution.py:17
  321.7 4.1 collective-permute-start.23
  368.5 6.5 %collective-permute-start.24 = (f32[1,200,128]{2,1,0:T(8,128)S(1)}, f32[1,200,128]{2,1,0:T(8,128)S(1)}, u32[]{:S(2)}, u32[]{:S(2)}) collective-permute-start(f32[1,200,128]{2,1,0:T(8,128)S(1)} %get-tuple-element.40), channel_id=1, source_target_pairs={{0,8},{8,16},{16,24},{24,0},{1,9},{9,17},{17,25},{25,1},{2,10},{10... | collective-permute-start | bytes 307208 | tf_op jit(solution)/shard_map/ppermute | solution.py:17
  370.7 5.0 %collective-permute-start.25 = (f32[1,200,128]{2,1,0:T(8,128)S(1)}, f32[1,200,128]{2,1,0:T(8,128)S(1)}, u32[]{:S(2)}, u32[]{:S(2)}) collective-permute-start(f32[1,200,128]{2,1,0:T(8,128)S(1)} %get-tuple-element.39), channel_id=1, source_target_pairs={{0,1},{1,2},{2,3},{3,4},{4,5},{5,6},{6,7},{7,0},{8,9},{9,10},{10,1... | collective-permute-start | bytes 307208 | tf_op jit(solution)/shard_map/ppermute | solution.py:17
  376.9 4.7 %collective-permute-start.26 = (f32[1,200,128]{2,1,0:T(8,128)S(1)}, f32[1,200,128]{2,1,0:T(8,128)S(1)}, u32[]{:S(2)}, u32[]{:S(2)}) collective-permute-start(f32[1,200,128]{2,1,0:T(8,128)S(1)} %get-tuple-element.14), channel_id=1, source_target_pairs={{0,24},{8,0},{16,8},{24,16},{1,25},{9,1},{17,9},{25,17},{2,26},{10... | collective-permute-start | bytes 307208 | tf_op jit(solution)/shard_map/ppermute | solution.py:17
  (28 other events, 780.5 us)
